TPU v7x, 32 devices: a whole 2x2x4 slice. The times are simulated.
32 devices in a mesh: doc: 2 (over x), seq: 4 (over y, core), head: 4 (over z).
Axes of the slice: x: 2, y: 2, z: 4, core: 2. Of those that a mesh axis runs over, the one named last changes fastest.
Arguments:
- length: int32 [2], P('doc'), parts along dimension 0, may hold values from 896 to 1024
- residual: bfloat16 [2048, 4096], P(('doc', 'seq'), 'head'), parts along dimension 0, may hold values from -6 to 6
- ssm_input: bfloat16 [2048, 4096], P(('doc', 'seq'), 'head'), parts along dimension 0, may hold values from -6 to 6
- state_in: bfloat16 [2048, 128], P(('doc', 'seq')), parts along dimension 0, may hold values from -6 to 6
- state_out: bfloat16 [2048, 128], P(('doc', 'seq')), parts along dimension 0, may hold values from -0.5 to 0.5
- step_raw: float32 [128, 1024], P(('doc', 'head'), 'seq'), parts along dimension 0, may hold values from -5 to 2
- decay_rate: float32 [64], P('head'), may hold values from 0 to 1, as said below
- ssm_gain: float32 [4096], P('head'), may hold values from 0.1 to 1.9
- out_weight: bfloat16 [4096, 4096], P('head'), may hold values from -0.09375 to 0.09375
- norm_gain: float32 [4096], replicated, may hold values from 0.1 to 1.9
- query_weight: bfloat16 [4096, 4096], P(None, 'head'), may hold values from -2 to 2
- key_weight: bfloat16 [4096, 1024], P(None, 'head'), may hold values from -3 to 3
- value_weight: bfloat16 [4096, 1024], P(None, 'head'), may hold values from -0.09375 to 0.09375
Outputs:
- layer_out: bfloat16 [2048, 4096], P(('doc', 'seq'), 'head'), parts along dimension 0
- head_out: bfloat16 [2048, 4096], P(('doc', 'seq'), 'head'), parts along dimension 0
There are 2 independent parts, one for each index of `doc`. A program takes and returns all parts, laid end to end along the dimension named above; an argument that names none is the same for every part. Nothing has to cross between parts.
Inputs may be any that keep to these rules, and one draw needn't show every extreme that they name: The document fills positions 0 to length - 1 of the 1024; later positions are padding. `decay_rate`: positive.
All inputs are finite; a program needn't handle non-finite values.
Results may differ from a plain program's by a relative error of at most 0.028.
The roundings to bfloat16 on the way count: a program that leaves them out, or rounds other values in their place, can miss the bound.
Values may be sent and summed in bfloat16 or wider, within the bound.
A program may use at most 64 MiB of HBM per device.

v0:
```python
import jax
import jax.numpy as jnp
from jax import lax
from jax.sharding import PartitionSpec as P

HEAD_DIM = 128
EPSILON = 1e-05
NEG_BIG = -1e30
HIGHEST = lax.Precision.HIGHEST


def prefix_2(value, axis, join, neutral):
    count, mine = (lax.axis_size(axis), lax.axis_index(axis))
    pieces = jax.tree.map(lambda part: lax.all_gather(part, axis), value)
    so_far = jax.tree.map(
        lambda part, zero: jnp.full_like(part, 0) + jnp.asarray(zero, part.dtype), value, neutral
    )

    def turn(position, so_far):
        longer = join(so_far, jax.tree.map(lambda part: part[position], pieces))
        return jax.tree.map(lambda new, old: jnp.where(position < mine, new, old), longer, so_far)

    return lax.fori_loop(0, count - 1, turn, so_far)


def chain_link(earlier, later):
    return (earlier[0] * later[0], later[0][:, None, None] * earlier[1] + later[1])


def body(
    length,
    residual,
    ssm_input,
    state_in,
    state_out,
    step_raw,
    decay_rate,
    ssm_gain,
    out_weight,
    norm_gain,
    query_weight,
    key_weight,
    value_weight,
):
    rows = residual.shape[0]
    local_heads = decay_rate.shape[0]
    head_width = ssm_input.shape[1] // local_heads
    seq_index = lax.axis_index("seq")
    limit = length[0]
    positions = seq_index * rows + jnp.arange(rows, dtype=jnp.int32)
    live_rows = positions < limit
    live = live_rows.astype(jnp.float32)
    delta = live[None, :] * jax.nn.softplus(step_raw)
    cumlog = jnp.cumsum(-decay_rate[:, None] * delta, axis=1)
    inputs = ssm_input.astype(jnp.float32).reshape(rows, local_heads, head_width)
    inner = jnp.dot(state_out, state_in.T, preferred_element_type=jnp.float32)
    causal = jnp.arange(rows)[:, None] >= jnp.arange(rows)[None, :]
    spread = cumlog[:, :, None] - cumlog[:, None, :]
    mixing = (
        jnp.where(causal[None], jnp.exp(jnp.where(causal[None], spread, 0.0)), 0.0)
        * inner[None]
        * delta[:, None, :]
    )
    within = jnp.einsum("hts,shp->thp", mixing, inputs, precision=HIGHEST)
    tail = jnp.exp(cumlog[:, -1:] - cumlog) * delta
    local_state = jnp.einsum(
        "hs,shp,sn->hpn", tail, inputs, state_in.astype(jnp.float32), precision=HIGHEST
    )
    block_decay = jnp.exp(cumlog[:, -1])
    prefix = prefix_2(
        (block_decay, local_state),
        "seq",
        chain_link,
        (jnp.ones_like(block_decay), jnp.zeros_like(local_state)),
    )
    incoming = prefix[1]
    carried = jnp.einsum("hpn,tn->thp", incoming, state_out.astype(jnp.float32), precision=HIGHEST)
    ssm_out = (within + jnp.exp(cumlog).T[:, :, None] * carried) * live[:, None, None]
    mean_square = jnp.mean(ssm_out * ssm_out, axis=2, keepdims=True)
    normed = (
        ssm_out * lax.rsqrt(mean_square + EPSILON) * ssm_gain.reshape(local_heads, head_width)
    ).astype(jnp.bfloat16)
    normed = normed.reshape(rows, local_heads * head_width)
    partial_value = jnp.dot(normed, out_weight, preferred_element_type=jnp.float32)
    model_width = norm_gain.shape[0]
    own_width = residual.shape[1]
    projected = lax.psum_scatter(partial_value, "head", scatter_dimension=1, tiled=True)
    layer_out = (residual.astype(jnp.float32) + projected).astype(jnp.bfloat16)
    widened = layer_out.astype(jnp.float32)
    squares = lax.psum(jnp.sum(widened * widened, axis=1), "head")
    piece_gain = lax.dynamic_slice_in_dim(norm_gain, lax.axis_index("head") * own_width, own_width)
    scaled = (widened * lax.rsqrt(squares / model_width + EPSILON)[:, None] * piece_gain).astype(
        jnp.bfloat16
    )
    attn_in = lax.all_gather(scaled, "head", axis=1, tiled=True)
    queries = jnp.dot(attn_in, query_weight, preferred_element_type=jnp.float32).astype(
        jnp.bfloat16
    )
    keys = jnp.dot(attn_in, key_weight, preferred_element_type=jnp.float32).astype(jnp.bfloat16)
    values = jnp.dot(attn_in, value_weight, preferred_element_type=jnp.float32).astype(jnp.bfloat16)
    query_local = query_weight.shape[1] // HEAD_DIM
    kv_local = key_weight.shape[1] // HEAD_DIM
    group_size = query_local // kv_local
    grouped = queries.reshape(rows, kv_local, group_size, HEAD_DIM)
    best = jnp.full((rows, query_local), NEG_BIG, jnp.float32)
    key_piece = lax.all_gather(keys, "seq", axis=0, tiled=True)
    value_piece = lax.all_gather(values, "seq", axis=0, tiled=True)
    count = key_piece.shape[0]
    key_pos = jnp.arange(count, dtype=jnp.int32)
    allowed = (key_pos[None, :] <= positions[:, None]) & (key_pos[None, :] < limit)
    scores = jnp.einsum(
        "tkgd,rkd->tkgr",
        grouped,
        key_piece.reshape(count, kv_local, HEAD_DIM),
        preferred_element_type=jnp.float32,
    ) * HEAD_DIM ** (-0.5)
    scores = scores.reshape(rows, query_local, count)
    allowed_wide = allowed[:, None, :]
    masked = jnp.where(allowed_wide, scores, NEG_BIG)
    new_best = jnp.maximum(best, jnp.max(masked, axis=2))
    weights = jnp.where(allowed_wide, jnp.exp(masked - new_best[:, :, None]), 0.0)
    total = jnp.sum(weights, axis=2)
    update = jnp.einsum(
        "tkgr,rkd->tkgd",
        weights.astype(jnp.bfloat16).reshape(rows, kv_local, group_size, count),
        value_piece.reshape(count, kv_local, HEAD_DIM),
        preferred_element_type=jnp.float32,
    )
    accum = update.reshape(rows, query_local, HEAD_DIM)
    folded = (new_best, total, accum)
    total = folded[1]
    accum = folded[2]
    safe_total = jnp.where(live_rows[:, None], total, 1.0)
    head_out = (
        (accum / safe_total[:, :, None] * live[:, None, None])
        .astype(jnp.bfloat16)
        .reshape(rows, query_local * HEAD_DIM)
    )
    return (layer_out, head_out)


def solution(mesh):
    placed = (
        P("doc"),
        P(("doc", "seq"), "head"),
        P(("doc", "seq"), "head"),
        P(("doc", "seq"), None),
        P(("doc", "seq"), None),
        P(("doc", "head"), "seq"),
        P("head"),
        P("head"),
        P("head", None),
        P(),
        P(None, "head"),
        P(None, "head"),
        P(None, "head"),
    )
    return jax.shard_map(
        body,
        mesh=mesh,
        in_specs=placed,
        out_specs=(P(("doc", "seq"), "head"), P(("doc", "seq"), "head")),
        check_vma=False,
    )
```

profile of v0, /device:TPU:0, one launch (start us, length us, event | category | flops | bytes accessed | tf_op | source)
XLA Modules:
  0.0 233.8 jit_solution(13353778681474807331)
XLA Ops:
  7.2 0.0 copy-start
  7.2 0.0 all-gather.7.cloned.1.call-start
  8.0 0.7 neg.8
  8.7 0.8 multiply_bitcast_fusion.1
  9.5 0.6 reduce-window.6
  10.0 0.2 slice_reduce_fusion
  10.2 0.1 copy_bitcast_fusion
  10.3 0.2 slice_reduce_fusion.1
  10.5 1.2 copy.34
  11.8 0.1 exponential_bitcast_fusion
  11.9 2.3 fusion.31
  14.2 0.0 all-gather.7.cloned.1.call-update
  14.2 0.0 reduce-scatter.2.cloned.1.call-start
  14.2 0.8 mul.159
  15.0 1.2 dynamic-slice
  16.9 0.2 dynamic-update-slice
  17.1 8.4 %all-reduce = f32[64]{0:T(128)S(1)} all-reduce(f32[64]{0:T(128)S(1)} %dynamic-update-slice), channel_id=2, replica_groups=mesh['doc'=2,'seq'=4,'head'=4] {'seq'}, use_global_device_ids=true, to_apply=%add | all-reduce | flops 64 | bytes 512
  25.5 0.1 reshape.196
  25.6 1.1 fusion.48
  26.7 4.4 %fusion.20 = f32[256,16,64]{0,2,1:T(8,128)} fusion(bf16[256,16,64]{0,2,1:T(8,128)(2,1)S(1)} %bitcast.100, f32[16,256]{1,0:T(8,128)S(1)} %get-tuple-element.130, f32[256,256]{1,0:T(8,128)S(1)} %fusion.48, f32[16,256]{1,0:T(8,128)S(1)} %copy_bitcast_fusion, pred[256,256]{1,0:T(8,128)(4,1)S(1)} %iota_compare_fusion.1), kind=kOutput, calls=%fused_computation.24 | convolution fusion | flops 810549248 | bytes 1933312 | tf_op jit(solution)/shard_map/hts,shp->thp/dot_general | solution.py:64
  31.1 0.0 copy-start.3
  31.1 8.5 %all-gather.7.cloned.1.call-done = f32[64,64,128]{2,1,0:T(8,128)} async-done(((f32[16,64,128]{2,1,0:T(8,128)}), f32[64,64,128]{2,1,0:T(8,128)}) %all-gather.7.cloned.1.call-update) | async-done | bytes 2097168 | tf_op jit(solution)/shard_map/all_gather | solution.py:14
  39.6 3.6 %while.14 = (s32[]{:T(128)}, f32[16,64,128]{2,1,0:T(8,128)S(1)}, s32[]{:T(128)}, f32[4,16]{1,0:T(4,128)S(1)}, f32[4,16,64,128]{3,2,1,0:T(8,128)}, /*index=5*/s32[]{:T(128)}, s32[]{:T(128)}) while((s32[]{:T(128)}, f32[16,64,128]{2,1,0:T(8,128)S(1)}, s32[]{:T(128)}, f32[4,16]{1,0:T(4,128)S(1)}, f32[4,16,64,128]{3,2,1,0:T(8,128)}, ...), condition=%wide.region_3.4_spmd.clone, body=%wide.region_2.3_spmd.clone.sunk | while | flops 524292 | bytes 1573169 | solution.py:23
  39.6 1.2 fusion.64
  40.8 1.2 fusion.64
  42.1 1.2 fusion.64
  43.2 0.0 copy-done.3
  43.2 1.9 multiply_reduce_fusion
  45.1 0.2 multiply_convert_fusion
  45.4 7.7 %fusion.49 = f32[256,4096]{1,0:T(8,128)} fusion(bf16[256,1024]{0,1:T(8,128)(2,1)S(1)} %bitcast.98, bf16[1024,4096]{1,0:T(8,128)(2,1)} %param.23), kind=kOutput, calls=%fused_computation.78 | convolution fusion | flops 2147483648 | bytes 13107200 | tf_op jit(solution)/shard_map/dot_general | solution.py:84
  53.0 0.0 copy-start.2
  53.0 0.0 reduce-scatter.2.cloned.1.call-update
  53.1 0.0 all-gather.5.cloned.1.call-start
  53.1 0.7 dynamic_slice.17
  53.9 76.2 %reduce-scatter.2.cloned.1.call-done = f32[256,1024]{1,0:T(8,128)} async-done(((f32[256,4096]{1,0:T(8,128)}), f32[256,1024]{1,0:T(8,128)}) %reduce-scatter.2.cloned.1.call-update) | async-done | bytes 1048592 | tf_op jit(solution)/shard_map/reduce_scatter | solution.py:87
  130.0 0.0 copy-done.2
  130.0 1.5 fusion.26
  131.5 0.0 copy-start.1
  131.5 11.0 %psum.7 = f32[256]{0:T(256)S(1)} all-reduce(f32[256]{0:T(256)S(1)} %get-tuple-element.127), channel_id=1, replica_groups=mesh['doc'=2,'seq'=4,'head'=4] {'head'}, use_global_device_ids=true, to_apply=%region_7.8 | all-reduce | flops 256 | bytes 2048 | tf_op jit(solution)/shard_map/psum | solution.py:90
  142.5 1.0 fusion.28
  143.5 0.0 all-gather.5.cloned.1.call-update
  143.5 0.2 fusion.34
  143.8 43.9 %all-gather.5.cloned.1.call-done = bf16[256,4096]{1,0:T(8,128)(2,1)} async-done(((bf16[256,1024]{1,0:T(8,128)(2,1)}), bf16[256,4096]{1,0:T(8,128)(2,1)}) %all-gather.5.cloned.1.call-update) | async-done | bytes 2097168 | tf_op jit(solution)/shard_map/all_gather | solution.py:95
  187.7 6.3 %convolution_convert_fusion = bf16[256,1024]{1,0:T(8,128)(2,1)S(1)} fusion(bf16[256,4096]{1,0:T(8,128)(2,1)} %all-gather.5.cloned.1.call-done, bf16[4096,1024]{1,0:T(8,128)(2,1)} %param.25), kind=kOutput, calls=%fused_computation.30 | convolution fusion | flops 2147745792 | bytes 11010048 | tf_op jit(solution)/shard_map/dot_general | solution.py:96
  194.0 0.0 copy-done.1
  194.0 1.2 reshape.194
  195.2 0.0 copy-done
  195.2 2.3 convolution_convert_fusion.2
  197.5 7.2 %all_gather.23 = bf16[1024,256]{1,0:T(8,128)(2,1)S(1)} all-gather(bf16[256,256]{1,0:T(8,128)(2,1)S(1)} %convolution_convert_fusion.2), channel_id=1, replica_groups=mesh['doc'=2,'seq'=4,'head'=4] {'seq'}, dimensions={0}, use_global_device_ids=true | all-gather | bytes 655360 | tf_op jit(solution)/shard_map/all_gather | solution.py:107
  204.6 0.2 copy.44
  204.9 2.9 %convolution_convert_fusion.1 = bf16[256,256]{1,0:T(8,128)(2,1)S(1)} fusion(bf16[256,4096]{1,0:T(8,128)(2,1)} %all-gather.5.cloned.1.call-done, bf16[4096,256]{1,0:T(8,128)(2,1)} %param.26), kind=kOutput, calls=%fused_computation.31 | convolution fusion | flops 536936448 | bytes 4325376 | tf_op jit(solution)/shard_map/dot_general | solution.py:99
  207.8 7.5 %all_gather.24 = bf16[1024,256]{1,0:T(8,128)(2,1)S(1)} all-gather(bf16[256,256]{1,0:T(8,128)(2,1)S(1)} %convolution_convert_fusion.1), channel_id=1, replica_groups=mesh['doc'=2,'seq'=4,'head'=4] {'seq'}, dimensions={0}, use_global_device_ids=true | all-gather | bytes 655360 | tf_op jit(solution)/shard_map/all_gather | solution.py:106
  215.3 0.9 reshape.193
  216.2 2.7 %fusion.1 = (f32[256,2,4]{0,2,1:T(4,128)S(1)}, f32[2,1024,256,4]{2,1,3,0:T(8,128)S(1)}) fusion(pred[256,1024]{0,1:T(8,128)(4,1)S(1)} %fusion.34, bf16[256,2,4,128]{3,2,1,0:T(4,128)(2,1)} %reshape.194, bf16[1024,2,128,1]{2,1,0,3:T(2,128)(2,1)} %bitcast.103), kind=kOutput, calls=%fused_computation.5 | convolution fusion | flops 543160320 | bytes 9707520 | tf_op jit(solution)/shard_map/tkgd,rkd->tkgr/dot_general | solution.py:111
  218.9 2.0 fusion.2
  220.9 3.2 %fusion.11 = f32[2,128,256,4]{2,1,3,0:T(8,128)} fusion(bf16[1024,2,128,1]{0,2,3,1:T(8,128)(2,1)S(1)} %bitcast.102, f32[2,1024,256,4]{2,1,3,0:T(8,128)S(1)} %get-tuple-element.138, f32[256,2,4]{0,2,1:T(4,128)S(1)} %broadcast_maximum_fusion, pred[256,1024]{0,1:T(8,128)(4,1)S(1)} %fusion.34), kind=kOutput, calls=%fused_computation.15 | convolution fusion | flops 547356672 | bytes 10231808 | tf_op jit(solution)/shard_map/tkgr,rkd->tkgd/dot_general | solution.py:123
  224.1 1.6 copy.40
  225.7 0.1 copy.39
  225.9 0.3 div.27
  226.2 1.0 fusion.30
  (17 shorter events, 0.2 us)
Async XLA Ops:
  7.2 188.0 %copy-start = (bf16[4096,256]{1,0:T(8,128)(2,1)S(1)}, bf16[4096,256]{1,0:T(8,128)(2,1)}, u32[]{:S(2)}) copy-start(bf16[4096,256]{1,0:T(8,128)(2,1)} %param.27) | copy-start | bytes 6291460
  7.2 32.4 %all-gather.7.cloned.1.call-start = ((), (), s32[]{:S(2)}) async-start(), calls=%async_computation.3 | async-start | bytes 2621440 | tf_op jit(solution)/shard_map/all_gather | solution.py:14
  14.2 115.8 %reduce-scatter.2.cloned.1.call-start = ((), (), s32[]{:S(2)}) async-start(), calls=%async_computation.1 | async-start | bytes 5242880 | tf_op jit(solution)/shard_map/reduce_scatter | solution.py:87
  31.1 12.2 %copy-start.3 = (bf16[256,128]{1,0:T(8,128)(2,1)S(1)}, bf16[256,128]{1,0:T(8,128)(2,1)}, u32[]{:S(2)}) copy-start(bf16[256,128]{1,0:T(8,128)(2,1)} %param.19) | copy-start | bytes 196612
  53.0 77.0 %copy-start.2 = (bf16[256,1024]{1,0:T(8,128)(2,1)S(1)}, bf16[256,1024]{1,0:T(8,128)(2,1)}, u32[]{:S(2)}) copy-start(bf16[256,1024]{1,0:T(8,128)(2,1)} %param.16) | copy-start | bytes 1572868
  53.1 134.6 %all-gather.5.cloned.1.call-start = ((), (), s32[]{:S(2)}) async-start(), calls=%async_computation.2 | async-start | bytes 2621440 | tf_op jit(solution)/shard_map/all_gather | solution.py:95
  131.5 62.5 %copy-start.1 = (bf16[256,1024]{1,0:T(8,128)(2,1)}, bf16[256,1024]{1,0:T(8,128)(2,1)S(1)}, u32[]{:S(2)}) copy-start(bf16[256,1024]{1,0:T(8,128)(2,1)S(1)} %get-tuple-element.128) | copy-start | bytes 1572868
Sparse Core Ops, SparseCore 0:
  14.3 25.2 all-gather.6
  53.2 76.7 reduce-scatter.1
  143.6 43.9 all-gather.4
where the time goes:
time: 235 us; the launch traced here: 234 us
  waiting for transfers between devices  129 us (55%)
  matrix products  34.8 us (15%)
  blocking collectives  34 us (14%)
  between operations  15.4 us (7%)
  other arithmetic  11.7 us (5%)
  local copies, waits for them, and re-layouts  9.02 us (4%)
    reduce_scatter x1, waiting for transfers between devices, body(): lax.psum_scatter(partial_value, 'head', scatter_dimension=1, tiled=True)  76.2 us
    all_gather x1, waiting for transfers between devices, body(): attn_in = lax.all_gather(scaled, 'head', axis=1, tiled=True)  43.9 us
    psum x1, blocking collectives, body(): squares = lax.psum(jnp.sum(widened * widened, axis=1), 'head')  11 us
    all_gather x1, waiting for transfers between devices, prefix_2(): pieces = jax.tree.map(lambda part: lax.all_gather(part, axis), value)  8.54 us
    unnamed x1, blocking collectives  8.37 us
    dot_general x1, matrix products, body(): jnp.dot(normed, out_weight, preferred_element_type=jnp.float32)  7.69 us
    all_gather x1, blocking collectives, body(): key_piece = lax.all_gather(keys, 'seq', axis=0, tiled=True)  7.46 us
    all_gather x1, blocking collectives, body(): value_piece = lax.all_gather(values, 'seq', axis=0, tiled=True)  7.15 us
  transfers between devices with their start and end apart: 3, of which 3 were waited for; matrix products, arithmetic and copies ran while one was open for 4% of the time, Pallas kernels for 0%

commit v1 on v0

--- a/solution.py
+++ b/solution.py
@@ -92,7 +92,12 @@
     scaled = (widened * lax.rsqrt(squares / model_width + EPSILON)[:, None] * piece_gain).astype(
         jnp.bfloat16
     )
-    attn_in = lax.all_gather(scaled, "head", axis=1, tiled=True)
+    ring = [scaled]
+    for hop in range(3):
+        ring.append(lax.ppermute(ring[-1], "head", [(dev, (dev + 1) % 4) for dev in range(4)]))
+    attn_in = jnp.roll(
+        jnp.concatenate(ring[::-1], axis=1), (lax.axis_index("head") + 1) * ring[0].shape[1], axis=1
+    )
     queries = jnp.dot(attn_in, query_weight, preferred_element_type=jnp.float32).astype(
         jnp.bfloat16
     )

time: 235 us -> 226 us (0.962)
  matrix products: 34.8 us -> 27 us
  waiting for transfers between devices: 129 us -> 123 us
  local copies, waits for them, and re-layouts: 9.02 us -> 14.5 us
    all_gather x1 -> x0, waiting for transfers between devices: 43.9 us -> none  [body(): attn_in = lax.all_gather(scaled, 'head', axis=1, tiled=True)]
    ppermute x0 -> x3, waiting for transfers between devices: none -> 38.3 us  [body(): lax.ppermute(ring[-1], 'head', [(dev, (dev + 1) % 4) for dev in range(4)])]
    unnamed x12 -> x24, local copies, waits for them, and re-layouts: 2.76 us -> 8.2 us
    dot_general x1, matrix products: 6.34 us -> 2.32 us  [body(): jnp.dot(attn_in, query_weight, preferred_element_type=jnp.float32)]
  transfers between devices with their start and end apart: 3 -> 5, of which waited for: 3 -> 5; matrix products, arithmetic and copies ran while one was open for 4% -> 4% of each run, Pallas kernels for 0% -> 0%
where the time goes in v1:
time: 226 us; the launch traced here: 225 us
  waiting for transfers between devices  123 us (54%)
  blocking collectives  33.6 us (15%)
  matrix products  27 us (12%)
  between operations  15.8 us (7%)
  local copies, waits for them, and re-layouts  14.5 us (6%)
  other arithmetic  11.3 us (5%)
    reduce_scatter x1, waiting for transfers between devices, body(): lax.psum_scatter(partial_value, 'head', scatter_dimension=1, tiled=True)  76.2 us
    ppermute x3, waiting for transfers between devices, body(): lax.ppermute(ring[-1], 'head', [(dev, (dev + 1) % 4) for dev in range(4)])  38.3 us
    psum x1, blocking collectives, body(): squares = lax.psum(jnp.sum(widened * widened, axis=1), 'head')  11 us
    all_gather x1, waiting for transfers between devices, prefix_2(): pieces = jax.tree.map(lambda part: lax.all_gather(part, axis), value)  8.54 us
    unnamed x1, blocking collectives  8.37 us
    unnamed x24, local copies, waits for them, and re-layouts  8.2 us
    dot_general x1, matrix products, body(): jnp.dot(normed, out_weight, preferred_element_type=jnp.float32)  7.69 us
    all_gather x1, blocking collectives, body(): key_piece = lax.all_gather(keys, 'seq', axis=0, tiled=True)  7.28 us
  transfers between devices with their start and end apart: 5, of which 5 were waited for; matrix products, arithmetic and copies ran while one was open for 4% of the time, Pallas kernels for 0%

profile of v1, /device:TPU:0, one launch (start us, length us, event | category | flops | bytes accessed | tf_op | source)
XLA Modules:
  0.0 225.4 jit_solution(4119998479374276725)
XLA Ops:
  7.2 0.0 copy-start
  7.2 0.0 all-gather.4.cloned.1.call-start
  8.0 0.7 neg.8
  8.7 0.8 multiply_bitcast_fusion.1
  9.5 0.6 reduce-window.6
  10.0 0.2 slice_reduce_fusion
  10.2 0.1 copy_bitcast_fusion
  10.3 0.2 slice_reduce_fusion.1
  10.5 1.2 copy.34
  11.8 0.1 exponential_bitcast_fusion
  11.9 2.3 %fusion.46 = f32[16,64,128]{2,1,0:T(8,128)} fusion(bf16[256,16,64]{0,2,1:T(8,128)(2,1)S(1)} %bitcast.96, f32[256,16]{0,1:T(8,128)S(1)} %get-tuple-element.134, bf16[256,128]{1,0:T(8,128)(2,1)} %param.18), kind=kOutput, calls=%fused_computation.49 | convolution fusion | flops 403177472 | bytes 1130496 | tf_op jit(solution)/shard_map/hs,shp,sn->hpn/dot_general | solution.py:66
  14.2 0.0 all-gather.4.cloned.1.call-update
  14.2 0.0 reduce-scatter.2.cloned.1.call-start
  14.2 0.8 mul.162
  15.0 1.2 dynamic-slice
  16.9 0.2 dynamic-update-slice
  17.1 8.4 %all-reduce = f32[64]{0:T(128)S(1)} all-reduce(f32[64]{0:T(128)S(1)} %dynamic-update-slice), channel_id=2, replica_groups=mesh['doc'=2,'seq'=4,'head'=4] {'seq'}, use_global_device_ids=true, to_apply=%add | all-reduce | flops 64 | bytes 512
  25.5 0.1 reshape.196
  25.6 1.1 fusion.66
  26.7 4.4 %fusion.26 = f32[256,16,64]{0,2,1:T(8,128)} fusion(bf16[256,16,64]{0,2,1:T(8,128)(2,1)S(1)} %bitcast.97, f32[16,256]{1,0:T(8,128)S(1)} %get-tuple-element.130, f32[256,256]{1,0:T(8,128)S(1)} %fusion.66, f32[16,256]{1,0:T(8,128)S(1)} %copy_bitcast_fusion, pred[256,256]{1,0:T(8,128)(4,1)S(1)} %iota_compare_fusion.1), kind=kOutput, calls=%fused_computation.30 | convolution fusion | flops 810549248 | bytes 1933312 | tf_op jit(solution)/shard_map/hts,shp->thp/dot_general | solution.py:64
  31.1 8.5 %all-gather.4.cloned.1.call-done = f32[64,64,128]{2,1,0:T(8,128)} async-done(((f32[16,64,128]{2,1,0:T(8,128)}), f32[64,64,128]{2,1,0:T(8,128)}) %all-gather.4.cloned.1.call-update) | async-done | bytes 2097168 | tf_op jit(solution)/shard_map/all_gather | solution.py:14
  39.6 3.6 %while.14 = (s32[]{:T(128)}, f32[16,64,128]{2,1,0:T(8,128)S(1)}, s32[]{:T(128)}, f32[4,16]{1,0:T(4,128)S(1)}, f32[4,16,64,128]{3,2,1,0:T(8,128)}, /*index=5*/s32[]{:T(128)}, s32[]{:T(128)}) while((s32[]{:T(128)}, f32[16,64,128]{2,1,0:T(8,128)S(1)}, s32[]{:T(128)}, f32[4,16]{1,0:T(4,128)S(1)}, f32[4,16,64,128]{3,2,1,0:T(8,128)}, ...), condition=%wide.region_3.4_spmd.clone, body=%wide.region_2.3_spmd.clone.sunk | while | flops 524292 | bytes 1573169 | solution.py:23
  39.6 1.2 fusion.79
  40.8 1.2 fusion.79
  42.1 1.2 fusion.79
  43.2 1.9 multiply_reduce_fusion
  45.1 0.2 multiply_convert_fusion
  45.3 7.7 %fusion.67 = f32[256,4096]{1,0:T(8,128)} fusion(bf16[256,1024]{0,1:T(8,128)(2,1)S(1)} %bitcast.95, bf16[1024,4096]{1,0:T(8,128)(2,1)} %param.23), kind=kOutput, calls=%fused_computation.95 | convolution fusion | flops 2147483648 | bytes 13107200 | tf_op jit(solution)/shard_map/dot_general | solution.py:84
  53.0 0.0 reduce-scatter.2.cloned.1.call-update
  53.1 0.7 dynamic_slice.21
  53.8 76.2 %reduce-scatter.2.cloned.1.call-done = f32[256,1024]{1,0:T(8,128)} async-done(((f32[256,4096]{1,0:T(8,128)}), f32[256,1024]{1,0:T(8,128)}) %reduce-scatter.2.cloned.1.call-update) | async-done | bytes 1048592 | tf_op jit(solution)/shard_map/reduce_scatter | solution.py:87
  130.0 1.5 fusion.41
  131.5 11.0 %psum.7 = f32[256]{0:T(256)S(1)} all-reduce(f32[256]{0:T(256)S(1)} %get-tuple-element.127), channel_id=1, replica_groups=mesh['doc'=2,'seq'=4,'head'=4] {'head'}, use_global_device_ids=true, to_apply=%region_7.8 | all-reduce | flops 256 | bytes 2048 | tf_op jit(solution)/shard_map/psum | solution.py:90
  142.5 0.2 fusion.43
  142.7 0.1 collective-permute-start
  142.8 13.6 %collective-permute-done = bf16[256,1024]{1,0:T(8,128)(2,1)S(1)} collective-permute-done((bf16[256,1024]{1,0:T(8,128)(2,1)S(1)}, bf16[256,1024]{1,0:T(8,128)(2,1)S(1)}, u32[]{:S(2)}, u32[]{:S(2)}) %collective-permute-start) | collective-permute-done | bytes 524320 | tf_op jit(solution)/shard_map/ppermute | solution.py:97
  156.3 12.8 %collective-permute-done.1 = bf16[256,1024]{1,0:T(8,128)(2,1)} collective-permute-done((bf16[256,1024]{1,0:T(8,128)(2,1)S(1)}, bf16[256,1024]{1,0:T(8,128)(2,1)}, u32[]{:S(2)}, u32[]{:S(2)}) %collective-permute-start.1) | collective-permute-done | bytes 524320 | tf_op jit(solution)/shard_map/ppermute | solution.py:97
  169.1 0.2 fusion.49
  169.4 11.9 %collective-permute-done.2 = bf16[256,1024]{1,0:T(8,128)(2,1)} collective-permute-done((bf16[256,1024]{1,0:T(8,128)(2,1)}, bf16[256,1024]{1,0:T(8,128)(2,1)}, u32[]{:S(2)}, u32[]{:S(2)}) %collective-permute-start.2) | collective-permute-done | bytes 524320 | tf_op jit(solution)/shard_map/ppermute | solution.py:97
  181.3 1.1 constant_dynamic-update-slice_fusion.7
  182.4 1.1 constant_dynamic-update-slice_fusion.6
  183.5 0.0 slice-start
  183.5 0.2 constant_dynamic-update-slice_fusion.4
  183.7 0.0 copy-start.4
  183.7 1.2 constant_dynamic-update-slice_fusion.3
  185.0 1.2 constant_dynamic-update-slice_fusion.2
  186.2 0.2 constant_dynamic-update-slice_fusion
  186.5 0.0 slice-start.1
  186.5 0.7 fusion.38
  187.2 0.7 fusion.35
  187.9 0.7 slice-done.1
  188.7 2.3 %fusion.32 = bf16[256,1024]{1,0:T(8,128)(2,1)S(1)} fusion(bf16[4096,1024]{1,0:T(8,128)(2,1)S(1)} %bitcast.103, bf16[256,8192]{1,0:T(8,128)(2,1)S(1)} %constant_dynamic-update-slice_fusion, s32[]{:T(128)S(6)} %select_n.74), kind=kOutput, calls=%fused_computation.36 | convolution fusion | flops 2147745792 | bytes 11010052 | tf_op jit(solution)/shard_map/dot_general | solution.py:101
  191.0 1.2 reshape.194
  192.2 6.9 %all_gather.19 = bf16[1024,256]{1,0:T(8,128)(2,1)S(1)} all-gather(bf16[256,256]{1,0:T(8,128)(2,1)S(1)} %fusion.35), channel_id=1, replica_groups=mesh['doc'=2,'seq'=4,'head'=4] {'seq'}, dimensions={0}, use_global_device_ids=true | all-gather | bytes 655360 | tf_op jit(solution)/shard_map/all_gather | solution.py:112
  199.1 0.2 copy.44
  199.3 7.3 %all_gather.20 = bf16[1024,256]{1,0:T(8,128)(2,1)S(1)} all-gather(bf16[256,256]{1,0:T(8,128)(2,1)S(1)} %fusion.38), channel_id=1, replica_groups=mesh['doc'=2,'seq'=4,'head'=4] {'seq'}, dimensions={0}, use_global_device_ids=true | all-gather | bytes 655360 | tf_op jit(solution)/shard_map/all_gather | solution.py:111
  206.6 0.9 reshape.193
  207.5 2.7 %fusion.1 = (f32[256,2,4]{0,2,1:T(4,128)S(1)}, f32[2,1024,256,4]{2,1,3,0:T(8,128)S(1)}) fusion(pred[256,1024]{0,1:T(8,128)(4,1)S(1)} %fusion.49, bf16[256,2,4,128]{3,2,1,0:T(4,128)(2,1)} %reshape.194, bf16[1024,2,128,1]{2,1,0,3:T(2,128)(2,1)} %bitcast.100), kind=kOutput, calls=%fused_computation.5 | convolution fusion | flops 543160320 | bytes 9707520 | tf_op jit(solution)/shard_map/tkgd,rkd->tkgr/dot_general | solution.py:116
  210.2 2.0 fusion.2
  212.2 3.2 %fusion.11 = f32[2,128,256,4]{2,1,3,0:T(8,128)} fusion(bf16[1024,2,128,1]{0,2,3,1:T(8,128)(2,1)S(1)} %bitcast.99, f32[2,1024,256,4]{2,1,3,0:T(8,128)S(1)} %get-tuple-element.138, f32[256,2,4]{0,2,1:T(4,128)S(1)} %broadcast_maximum_fusion, pred[256,1024]{0,1:T(8,128)(4,1)S(1)} %fusion.49), kind=kOutput, calls=%fused_computation.15 | convolution fusion | flops 547356672 | bytes 10231808 | tf_op jit(solution)/shard_map/tkgr,rkd->tkgd/dot_general | solution.py:128
  215.5 1.6 copy.40
  217.1 0.1 copy.39
  217.2 0.3 div.27
  217.5 1.0 fusion.45
  (31 shorter events, 0.2 us)
Async XLA Ops:
  7.2 179.3 %copy-start = (bf16[4096,256]{1,0:T(8,128)(2,1)S(1)}, bf16[4096,256]{1,0:T(8,128)(2,1)}, u32[]{:S(2)}) copy-start(bf16[4096,256]{1,0:T(8,128)(2,1)} %param.26) | copy-start | bytes 6291460
  7.2 32.4 %all-gather.4.cloned.1.call-start = ((), (), s32[]{:S(2)}) async-start(), calls=%async_computation.2 | async-start | bytes 2621440 | tf_op jit(solution)/shard_map/all_gather | solution.py:14
  14.2 115.8 %reduce-scatter.2.cloned.1.call-start = ((), (), s32[]{:S(2)}) async-start(), calls=%async_computation.1 | async-start | bytes 5242880 | tf_op jit(solution)/shard_map/reduce_scatter | solution.py:87
  31.1 12.2 %copy-start.3 = (bf16[256,128]{1,0:T(8,128)(2,1)S(1)}, bf16[256,128]{1,0:T(8,128)(2,1)}, u32[]{:S(2)}) copy-start(bf16[256,128]{1,0:T(8,128)(2,1)} %param.19) | copy-start | bytes 196612
  53.0 77.0 %copy-start.2 = (bf16[256,1024]{1,0:T(8,128)(2,1)S(1)}, bf16[256,1024]{1,0:T(8,128)(2,1)}, u32[]{:S(2)}) copy-start(bf16[256,1024]{1,0:T(8,128)(2,1)} %param.16) | copy-start | bytes 1572868
  131.5 54.8 %copy-start.1 = (bf16[256,1024]{1,0:T(8,128)(2,1)}, bf16[256,1024]{1,0:T(8,128)(2,1)S(1)}, u32[]{:S(2)}) copy-start(bf16[256,1024]{1,0:T(8,128)(2,1)S(1)} %get-tuple-element.128) | copy-start | bytes 1572868
  142.7 13.6 %collective-permute-start = (bf16[256,1024]{1,0:T(8,128)(2,1)S(1)}, bf16[256,1024]{1,0:T(8,128)(2,1)S(1)}, u32[]{:S(2)}, u32[]{:S(2)}) collective-permute-start(bf16[256,1024]{1,0:T(8,128)(2,1)S(1)} %fusion.43), channel_id=1, source_target_pairs={{0,1},{1,2},{2,3},{3,0},{4,5},{5,6},{6,7},{7,4},{8,9},{9,10},{10,1... | collective-permute-start | bytes 1572872 | tf_op jit(solution)/shard_map/ppermute | solution.py:97
  156.3 12.8 %collective-permute-start.1 = (bf16[256,1024]{1,0:T(8,128)(2,1)S(1)}, bf16[256,1024]{1,0:T(8,128)(2,1)}, u32[]{:S(2)}, u32[]{:S(2)}) collective-permute-start(bf16[256,1024]{1,0:T(8,128)(2,1)S(1)} %collective-permute-done), channel_id=1, source_target_pairs={{0,1},{1,2},{2,3},{3,0},{4,5},{5,6},{6,7},{7,4},{8,9},{9,10},{10,1... | collective-permute-start | bytes 1572872 | tf_op jit(solution)/shard_map/ppermute | solution.py:97
  169.1 12.2 %collective-permute-start.2 = (bf16[256,1024]{1,0:T(8,128)(2,1)}, bf16[256,1024]{1,0:T(8,128)(2,1)}, u32[]{:S(2)}, u32[]{:S(2)}) collective-permute-start(bf16[256,1024]{1,0:T(8,128)(2,1)} %collective-permute-done.1), channel_id=1, source_target_pairs={{0,1},{1,2},{2,3},{3,0},{4,5},{5,6},{6,7},{7,4},{8,9},{9,10},{10,1... | collective-permute-start | bytes 1572872 | tf_op jit(solution)/shard_map/ppermute | solution.py:97
  183.5 4.5 %slice-start = ((s8[8388608]{0:T(1024)(128)(4,1)}), s8[4194304]{0:T(1024)(128)(4,1)S(1)}, s32[]{:S(2)}) async-start(s8[8388608]{0:T(1024)(128)(4,1)} %bitcast.102), calls=%async_computation.3 | async-start | bytes 8388608
  183.7 3.5 %copy-start.4 = (bf16[4096,256]{1,0:T(8,128)(2,1)S(1)}, bf16[4096,256]{1,0:T(8,128)(2,1)}, u32[]{:S(2)}) copy-start(bf16[4096,256]{1,0:T(8,128)(2,1)} %param.27) | copy-start | bytes 6291460
  186.5 2.2 slice-start.1
Sparse Core Ops, SparseCore 0:
  14.3 25.2 all-gather.3
  53.2 76.7 reduce-scatter.1
